TPU v7x, 512 devices: a whole 4x4x16 slice. The times are simulated.
512 devices in a mesh: tm: 32 (over z, y_hi), lat: 16 (over x, y_lo, core).
Axes of the slice: x: 4, y: 4 (y_hi: 2, y_lo: 2; y = y_hi * 2 + y_lo), z: 16, core: 2. Of those that a mesh axis runs over, the one named last changes fastest.
Arguments:
- controls: float32 [32, 3, 512, 1024], P('tm', None, 'lat'), may hold values from -3 to 3
- background: float32 [3, 512, 1024], P(None, 'lat'), may hold values from -3 to 3
- observations: float32 [32, 4, 512, 1024], P('tm', None, 'lat'), may hold values from -3 to 3
- obs_count: int32 [32, 4, 512, 1024], P('tm', None, 'lat'), may hold values from 0 to 3
Outputs:
- slid_controls: float32 [32, 3, 512, 1024], P('tm', None, 'lat')
- gradient: float32 [32, 3, 512, 1024], P('tm', None, 'lat')
- cost: float32 [], replicated
All inputs are finite; a program needn't handle non-finite values.
Results may differ from a plain program's by a relative error of at most 0.0001.
Values sent between devices are 32-bit elements; how exact they have to be, the bound alone decides.
A program may use at most 64 MiB of HBM per device.

v0:
```python
import jax
import jax.numpy as jnp
from jax import lax
from jax.sharding import Mesh
from jax.sharding import PartitionSpec as P

LAT = ("lat_0", "lat_1", "lat_2")
TM = ("tm_0", "tm_1")
TM_LAT = ("tm_0", "tm_1", "lat_0", "lat_1", "lat_2")
courant = 0.25
diffusion = 0.1
spin_scale = 0.3
obs_weight = 0.5
q_weight = 1.0
step_scale = 0.2
epsilon = 1e-06


def extended_2(cells, sides, width):
    for axis, dim in sides:
        count = lax.axis_size(axis)
        ends = count - 1
        head = lax.slice_in_dim(cells, 0, width, axis=dim)
        tail = lax.slice_in_dim(cells, cells.shape[dim] - width, cells.shape[dim], axis=dim)
        cells = jnp.concatenate(
            [
                lax.ppermute(tail, axis, [(i, (i + 1) % count) for i in range(ends)]),
                cells,
                lax.ppermute(head, axis, [((i + 1) % count, i) for i in range(ends)]),
            ],
            axis=dim,
        )
    return cells


def from_behind(block, axis, distance):
    devices = range(lax.axis_size(axis))
    route = [(i - distance, i) for i in devices if i - distance in devices]
    return lax.ppermute(block, axis, route)


def by_axis(x, axes):
    for axis in axes:
        x = lax.psum(x, axis)
    return x


def advance(extended, coriolis):
    center = extended[:, 1:-1]
    north = extended[:, 2:]
    south = extended[:, :-2]
    east = jnp.roll(center, -1, axis=2)
    west = jnp.roll(center, 1, axis=2)
    height, zonal, merid = (center[0], center[1], center[2])
    flux_east = east[1] * (1.0 + east[0])
    flux_west = west[1] * (1.0 + west[0])
    flux_north = north[2] * (1.0 + north[0])
    flux_south = south[2] * (1.0 + south[0])
    spread = north + south + east + west - 4.0 * center
    half = 0.5 * courant
    new_height = (
        height - half * (flux_east - flux_west + flux_north - flux_south) + diffusion * spread[0]
    )
    new_zonal = (
        zonal
        - half * (east[0] - west[0])
        + coriolis * merid
        - half * (zonal * (east[1] - west[1]) + merid * (north[1] - south[1]))
        + diffusion * spread[1]
    )
    new_merid = (
        merid
        - half * (north[0] - south[0])
        - coriolis * zonal
        - half * (zonal * (east[2] - west[2]) + merid * (north[2] - south[2]))
        + diffusion * spread[2]
    )
    return jnp.stack([new_height, new_zonal, new_merid])


def coriolis_rows(index, total):
    latitude = jnp.pi * ((index.astype(jnp.float32) + 0.5) / total - 0.5)
    return (spin_scale * jnp.sin(latitude))[:, None]


def section_rows(current, first, margin, total):
    count = current.shape[1] - 2
    index = first - margin + jnp.arange(count, dtype=jnp.int32)
    valid = ((index >= 0) & (index < total)).astype(jnp.float32)[:, None]
    return advance(current, coriolis_rows(index, total)) * valid


def add_rims(wide, got, width):
    inner = wide[:, width:-width]
    count = inner.shape[1]
    lower = jnp.pad(got[:, :width], ((0, 0), (0, count - width), (0, 0)))
    upper = jnp.pad(got[:, -width:], ((0, 0), (count - width, 0), (0, 0)))
    return inner + lower + upper


def with_height(grad, inject):
    return grad + jnp.concatenate([inject[None], jnp.zeros_like(grad[1:])], axis=0)


def forward_deep(state, weights, targets, first, total):
    rows = state.shape[1]
    steps = targets.shape[0]
    current = extended_2(state, ((LAT, 1),), steps)
    inputs = []
    resids = []
    cost = jnp.zeros((), jnp.float32)
    for section in range(steps):
        margin = steps - 1 - section
        inputs.append(current)
        current = section_rows(current, first, margin, total)
        resid = current[0, margin : margin + rows] - targets[section]
        resids.append(weights[section] * resid)
        cost = cost + 0.5 * jnp.sum(weights[section] * resid * resid)
    return (current, cost, inputs, resids)


def backward_deep(start_grad, inputs, resids, first, total):
    steps = len(inputs)
    grad = start_grad
    for section in reversed(range(steps)):
        margin = steps - 1 - section
        grad = with_height(grad, jnp.pad(resids[section], ((margin, margin), (0, 0))))
        outputs, pull = jax.vjp(
            lambda current: section_rows(current, first, margin, total), inputs[section]
        )
        grad = pull(grad)[0]
    rims = jnp.concatenate([grad[:, :steps], grad[:, -steps:]], axis=1)
    got = extended_2(rims, ((LAT, 1),), steps)
    return add_rims(grad, got, steps)


def per_device(controls, background, observations, obs_count):
    state = controls[0]
    rows = state.shape[1]
    total = rows * lax.axis_size(LAT)
    first = lax.axis_index(LAT) * rows
    position = lax.axis_index(TM)
    windows = lax.axis_size(TM)
    weights = obs_weight * obs_count[0].astype(jnp.float32)
    targets = observations[0]
    following = from_behind(state, TM, -1)
    final, obs_cost, inputs, resids = forward_deep(state, weights, targets, first, total)
    received = from_behind(final, TM, 1)
    previous = jnp.where(position == 0, background, received)
    misfit = state - previous
    weighted = q_weight * misfit
    local_cost = obs_cost + 0.5 * q_weight * jnp.sum(misfit * misfit)
    later = jnp.where(
        position == windows - 1, jnp.zeros_like(final), q_weight * (following - final)
    )
    cost_total = by_axis(local_cost, TM_LAT)
    adjoint = backward_deep(-later, inputs, resids, first, total)
    gradient = weighted + adjoint
    squares = jnp.sum(gradient * gradient)
    square_total = by_axis(squares, TM_LAT)
    entries = float(windows * lax.axis_size(LAT) * state.size)
    norm = jnp.sqrt(square_total / entries + epsilon)
    updated = state - step_scale * gradient / norm
    arriving = from_behind(updated, TM, -1)
    slid = jnp.where(position == windows - 1, final, arriving)
    return (slid[None], gradient[None], cost_total)


def solution(mesh):
    finer = Mesh(mesh.devices.reshape(16, 2, 4, 2, 2), ("tm_0", "tm_1", "lat_0", "lat_1", "lat_2"))
    return jax.shard_map(
        per_device,
        mesh=finer,
        in_specs=(
            P(TM, None, LAT, None),
            P(None, LAT, None),
            P(TM, None, LAT, None),
            P(TM, None, LAT, None),
        ),
        out_specs=(P(TM, None, LAT, None), P(TM, None, LAT, None), P()),
        check_vma=False,
    )
```

profile of v0, /device:TPU:16, one launch (start us, length us, event | category | flops | bytes accessed | tf_op | source)
XLA Modules:
  0.0 145.0 jit_solution(15232609845705432557)
XLA Ops:
  0.6 7.6 %collective-permute-start.3 = (f32[3,32,1024]{2,1,0:T(8,128)}, f32[3,32,1024]{2,1,0:T(8,128)}, u32[]{:S(2)}, u32[]{:S(2)}) collective-permute-start(f32[3,32,1024]{2,1,0:T(8,128)} %bitcast.92), channel_id=1, source_target_pairs={{16,0},{32,16},{48,32},{64,48},{80,64},{96,80},{112,96},{128,112},... | collective-permute-start | bytes 1179656 | tf_op jit(solution)/shard_map/ppermute | solution.py:39
  8.2 1.0 fusion.121
  9.2 1.3 collective-permute-start
  10.5 1.3 collective-permute-start.1
  12.6 1.9 %convert_multiply_fusion = f32[1,4,32,1024]{3,2,1,0:T(8,128)} fusion(s32[1,4,32,1024]{3,2,1,0:T(8,128)} %param.7), kind=kLoop, calls=%fused_computation.32 | loop fusion | flops 262144 | bytes 1048576 | tf_op jit(solution)/shard_map/mul | solution.py:144
  16.0 0.8 fusion.41
  17.9 0.8 fusion.38
  20.0 0.8 fusion.35
  22.4 0.8 fusion.63
  23.8 0.8 maximum_multiply_fusion.3
  24.7 1.9 %collective-permute-start.2 = (f32[3,32,1024]{2,1,0:T(8,128)}, f32[3,32,1024]{2,1,0:T(8,128)}, u32[]{:S(2)}, u32[]{:S(2)}) collective-permute-start(f32[3,32,1024]{2,1,0:T(8,128)} %maximum_multiply_fusion.3), channel_id=1, source_target_pairs={{0,16},{16,32},{32,48},{48,64},{64,80},{80,96},{96,112},{112,128},... | collective-permute-start | bytes 1179656 | tf_op jit(solution)/shard_map/ppermute | solution.py:39
  26.6 2.4 %fusion.50 = (f32[]{:T(128)}, f32[]{:T(128)}, f32[]{:T(128)}, f32[]{:T(128)}, f32[32,1024]{1,0:T(8,128)S(1)}, /*index=5*/f32[32,1024]{1,0:T(8,128)S(1)}, f32[32,1024]{1,0:T(8,128)}) fusion(f32[3,32,1024]{2,1,0:T(8,128)} %maximum_multiply_fusion.3, f32[1,4,32,1024]{3,2,1,0:T(8,128)S(1)} %copy-done.12, f32[1,4,32,1024]{3,2,1,0:T(8,128)S(1)} %copy-done.43, ...), kind=kLoop, calls=%fused_computation.234 | loop fusion | flops 524284 | bytes 1966096 | tf_op jit(solution)/shard_map/reduce_sum | solution.py:118
  32.9 0.9 pad_bitcast_fusion
  33.9 1.1 fusion.66
  35.1 1.2 add_multiply_fusion.3
  39.1 0.8 copy-done.48
  40.1 0.8 copy-done.5
  43.4 0.7 copy-done.47
  44.3 0.8 copy-done.1
  51.2 4.9 %collective-permute-start.4 = (f32[3,4,1024]{2,1,0:T(4,128)S(1)}, f32[3,4,1024]{2,1,0:T(4,128)S(1)}, u32[]{:S(2)}, u32[]{:S(2)}) collective-permute-start(f32[3,4,1024]{2,1,0:T(4,128)S(1)} %get-tuple-element.72), channel_id=1, source_target_pairs={{0,1},{1,2},{2,3},{3,4},{4,5},{5,6},{6,7},{7,8},{8,9},{9,10},{10,1... | collective-permute-start | bytes 147464 | tf_op jit(solution)/shard_map/ppermute | solution.py:27
  56.1 1.4 collective-permute-start.5
  57.7 1.7 %multiply_reduce_fusion = (f32[]{:T(128)}, f32[3,32,1024]{2,1,0:T(8,128)S(1)}) fusion(f32[3,32,1024]{2,1,0:T(8,128)S(1)} %copy-done.50, f32[3,32,1024]{2,1,0:T(8,128)} %collective-permute-done.2, pred[]{:T(512)S(6)} %eq.8, f32[1,3,32,1024]{3,2,1,0:T(8,128)S(1)} %copy-done.11), kind=kLoop, calls=%fused_computation.101 | loop fusion | flops 393215 | bytes 1572869 | tf_op jit(solution)/shard_map/reduce_sum | solution.py:152
  60.1 1.8 %collective-permute-done.5 = f32[3,4,1024]{2,1,0:T(4,128)S(1)} collective-permute-done((f32[3,4,1024]{2,1,0:T(4,128)S(1)}, f32[3,4,1024]{2,1,0:T(4,128)S(1)}, u32[]{:S(2)}, u32[]{:S(2)}) %collective-permute-start.5) | collective-permute-done | bytes 49184 | tf_op jit(solution)/shard_map/ppermute | solution.py:29
  61.9 0.7 multiply_reduce_fusion.1
  62.6 35.0 %all-reduce.137 = (f32[]{:T(128)}, f32[]{:T(128)}) all-reduce(f32[]{:T(128)} %get-tuple-element.22, f32[]{:T(128)S(6)} %add.788), channel_id=1, replica_groups=mesh['tm_0'=16,'tm_1'=2,'lat_0'=4,'lat_1'=2,'lat_2'=2] {'tm_0'}, use_global_device_ids=true, to_apply=%region_1.2 | all-reduce | flops 2 | bytes 16 | tf_op jit(solution)/shard_map/psum | solution.py:44
  97.6 7.1 %all-reduce.141 = (f32[]{:T(128)}, f32[]{:T(128)}) all-reduce(f32[]{:T(128)} %get-tuple-element.7, f32[]{:T(128)} %get-tuple-element.8), channel_id=1, replica_groups=mesh['tm_0'=16,'tm_1'=2,'lat_0'=4,'lat_1'=2,'lat_2'=2] {'tm_1'}, use_global_device_ids=true, to_apply=%region_2.3 | all-reduce | flops 2 | bytes 16 | tf_op jit(solution)/shard_map/psum | solution.py:44
  104.7 14.3 %all-reduce.138 = (f32[]{:T(128)}, f32[]{:T(128)}) all-reduce(f32[]{:T(128)} %get-tuple-element.15, f32[]{:T(128)} %get-tuple-element.16), channel_id=1, replica_groups=mesh['tm_0'=16,'tm_1'=2,'lat_0'=4,'lat_1'=2,'lat_2'=2] {'lat_0'}, use_global_device_ids=true, to_apply=%region_3.4 | all-reduce | flops 2 | bytes 16 | tf_op jit(solution)/shard_map/psum | solution.py:44
  119.0 5.6 %all-reduce.140 = (f32[]{:T(128)}, f32[]{:T(128)}) all-reduce(f32[]{:T(128)} %get-tuple-element.9, f32[]{:T(128)} %get-tuple-element.10), channel_id=1, replica_groups=mesh['tm_0'=16,'tm_1'=2,'lat_0'=4,'lat_1'=2,'lat_2'=2] {'lat_1'}, use_global_device_ids=true, to_apply=%region_4.5 | all-reduce | flops 2 | bytes 16 | tf_op jit(solution)/shard_map/psum | solution.py:44
  124.6 3.1 %all-reduce.139 = (f32[]{:T(128)}, f32[]{:T(128)}) all-reduce(f32[]{:T(128)} %get-tuple-element.13, f32[]{:T(128)} %get-tuple-element.14), channel_id=1, replica_groups=mesh['tm_0'=16,'tm_1'=2,'lat_0'=4,'lat_1'=2,'lat_2'=2] {'lat_2'}, use_global_device_ids=true, to_apply=%region_5.6 | all-reduce | flops 2 | bytes 16 | tf_op jit(solution)/shard_map/psum | solution.py:44
  128.5 2.2 %collective-permute-start.6 = (f32[3,32,1024]{2,1,0:T(8,128)S(1)}, f32[3,32,1024]{2,1,0:T(8,128)S(1)}, u32[]{:S(2)}, u32[]{:S(2)}) collective-permute-start(f32[3,32,1024]{2,1,0:T(8,128)S(1)} %divide_subtract_fusion), channel_id=1, source_target_pairs={{16,0},{32,16},{48,32},{64,48},{80,64},{96,80},{112,96},{128,112},... | collective-permute-start | bytes 1179656 | tf_op jit(solution)/shard_map/ppermute | solution.py:39
  130.7 13.4 %collective-permute-done.6 = f32[3,32,1024]{2,1,0:T(8,128)S(1)} collective-permute-done((f32[3,32,1024]{2,1,0:T(8,128)S(1)}, f32[3,32,1024]{2,1,0:T(8,128)S(1)}, u32[]{:S(2)}, u32[]{:S(2)}) %collective-permute-start.6) | collective-permute-done | bytes 393248 | tf_op jit(solution)/shard_map/ppermute | solution.py:39
  144.1 0.9 select_bitcast_fusion
  (211 shorter events, 19.4 us)
Async XLA Ops:
  0.6 34.4 %collective-permute-start.3 = (f32[3,32,1024]{2,1,0:T(8,128)}, f32[3,32,1024]{2,1,0:T(8,128)}, u32[]{:S(2)}, u32[]{:S(2)}) collective-permute-start(f32[3,32,1024]{2,1,0:T(8,128)} %bitcast.92), channel_id=1, source_target_pairs={{16,0},{32,16},{48,32},{64,48},{80,64},{96,80},{112,96},{128,112},... | collective-permute-start | bytes 1179656 | tf_op jit(solution)/shard_map/ppermute | solution.py:39
  9.2 5.9 %collective-permute-start = (f32[3,4,1024]{2,1,0:T(4,128)S(1)}, f32[3,4,1024]{2,1,0:T(4,128)S(1)}, u32[]{:S(2)}, u32[]{:S(2)}) collective-permute-start(f32[3,4,1024]{2,1,0:T(4,128)S(1)} %get-tuple-element.254), channel_id=1, source_target_pairs={{0,1},{1,2},{2,3},{3,4},{4,5},{5,6},{6,7},{7,8},{8,9},{9,10},{10,1... | collective-permute-start | bytes 147464 | tf_op jit(solution)/shard_map/ppermute | solution.py:27
  10.5 4.6 %collective-permute-start.1 = (f32[3,4,1024]{2,1,0:T(4,128)S(1)}, f32[3,4,1024]{2,1,0:T(4,128)S(1)}, u32[]{:S(2)}, u32[]{:S(2)}) collective-permute-start(f32[3,4,1024]{2,1,0:T(4,128)S(1)} %get-tuple-element.255), channel_id=1, source_target_pairs={{1,0},{2,1},{3,2},{4,3},{5,4},{6,5},{7,6},{8,7},{9,8},{10,9},{11,1... | collective-permute-start | bytes 147464 | tf_op jit(solution)/shard_map/ppermute | solution.py:29
  11.9 5.1 %copy-start.61 = (f32[38]{0:T(128)}, f32[38]{0:T(128)S(1)}, u32[]{:S(2)}) copy-start(f32[38]{0:T(128)S(1)} %and_convert_fusion.3) | copy-start | bytes 460
  11.9 6.9 %copy-start.52 = (f32[36]{0:T(128)}, f32[36]{0:T(128)S(1)}, u32[]{:S(2)}) copy-start(f32[36]{0:T(128)S(1)} %sine_multiply_fusion.2) | copy-start | bytes 436
  12.0 7.1 %copy-start.63 = (f32[36]{0:T(128)}, f32[36]{0:T(128)S(1)}, u32[]{:S(2)}) copy-start(f32[36]{0:T(128)S(1)} %and_convert_fusion.2) | copy-start | bytes 436
  12.0 8.8 %copy-start.54 = (f32[34]{0:T(128)}, f32[34]{0:T(128)S(1)}, u32[]{:S(2)}) copy-start(f32[34]{0:T(128)S(1)} %sine_multiply_fusion.1) | copy-start | bytes 412
  12.0 9.0 %copy-start.65 = (f32[34]{0:T(128)}, f32[34]{0:T(128)S(1)}, u32[]{:S(2)}) copy-start(f32[34]{0:T(128)S(1)} %and_convert_fusion.1) | copy-start | bytes 412
  12.6 2.5 %copy-start.10 = (f32[1,3,32,1024]{3,2,1,0:T(8,128)S(1)}, f32[1,3,32,1024]{3,2,1,0:T(8,128)}, u32[]{:S(2)}) copy-start(f32[1,3,32,1024]{3,2,1,0:T(8,128)} %param.4) | copy-start | bytes 1179652
  15.3 1.5 %copy-start.13 = (f32[3,38,1]{2,1,0:T(8,128)}, f32[3,38,1]{2,1,0:T(8,128)S(1)}, u32[]{:S(2)}) copy-start(f32[3,38,1]{2,1,0:T(8,128)S(1)} %get-tuple-element.228) | copy-start | bytes 1372
  17.2 1.6 %copy-start.15 = (f32[3,36,1]{2,1,0:T(8,128)}, f32[3,36,1]{2,1,0:T(8,128)S(1)}, u32[]{:S(2)}) copy-start(f32[3,36,1]{2,1,0:T(8,128)S(1)} %get-tuple-element.223) | copy-start | bytes 1300
  17.2 1.6 %copy-start.17 = (f32[3,36,1]{2,1,0:T(8,128)}, f32[3,36,1]{2,1,0:T(8,128)S(1)}, u32[]{:S(2)}) copy-start(f32[3,36,1]{2,1,0:T(8,128)S(1)} %get-tuple-element.224) | copy-start | bytes 1300
  17.5 1.3 copy-start
  19.2 1.6 %copy-start.19 = (f32[3,34,1]{2,1,0:T(8,128)}, f32[3,34,1]{2,1,0:T(8,128)S(1)}, u32[]{:S(2)}) copy-start(f32[3,34,1]{2,1,0:T(8,128)S(1)} %get-tuple-element.219) | copy-start | bytes 1228
  19.2 1.5 %copy-start.21 = (f32[3,34,1]{2,1,0:T(8,128)}, f32[3,34,1]{2,1,0:T(8,128)S(1)}, u32[]{:S(2)}) copy-start(f32[3,34,1]{2,1,0:T(8,128)S(1)} %get-tuple-element.220) | copy-start | bytes 1228
  21.2 1.9 %copy-start.32 = (f32[3,32,1]{2,1,0:T(8,128)}, f32[3,32,1]{2,1,0:T(8,128)S(1)}, u32[]{:S(2)}) copy-start(f32[3,32,1]{2,1,0:T(8,128)S(1)} %get-tuple-element.216) | copy-start | bytes 1156
  21.4 1.7 %copy-start.6 = (f32[3,32,1023]{2,1,0:T(8,128)}, f32[3,32,1023]{2,1,0:T(8,128)S(1)}, u32[]{:S(2)}) copy-start(f32[3,32,1023]{2,1,0:T(8,128)S(1)} %get-tuple-element.213) | copy-start | bytes 1178500
  21.4 1.7 %copy-start.8 = (f32[3,32,1023]{2,1,0:T(8,128)}, f32[3,32,1023]{2,1,0:T(8,128)S(1)}, u32[]{:S(2)}) copy-start(f32[3,32,1023]{2,1,0:T(8,128)S(1)} %get-tuple-element.214) | copy-start | bytes 1178500
  23.2 3.4 %copy-start.43 = (f32[1,4,32,1024]{3,2,1,0:T(8,128)S(1)}, f32[1,4,32,1024]{3,2,1,0:T(8,128)}, u32[]{:S(2)}) copy-start(f32[1,4,32,1024]{3,2,1,0:T(8,128)} %param.6) | copy-start | bytes 1572868
  23.4 1.3 copy-start.26
  23.4 3.3 %copy-start.12 = (f32[1,4,32,1024]{3,2,1,0:T(8,128)S(1)}, f32[1,4,32,1024]{3,2,1,0:T(8,128)}, u32[]{:S(2)}) copy-start(f32[1,4,32,1024]{3,2,1,0:T(8,128)} %convert_multiply_fusion) | copy-start | bytes 1572868
  24.7 33.0 %collective-permute-start.2 = (f32[3,32,1024]{2,1,0:T(8,128)}, f32[3,32,1024]{2,1,0:T(8,128)}, u32[]{:S(2)}, u32[]{:S(2)}) collective-permute-start(f32[3,32,1024]{2,1,0:T(8,128)} %maximum_multiply_fusion.3), channel_id=1, source_target_pairs={{0,16},{16,32},{32,48},{48,64},{64,80},{80,96},{96,112},{112,128},... | collective-permute-start | bytes 1179656 | tf_op jit(solution)/shard_map/ppermute | solution.py:39
  51.2 8.9 %collective-permute-start.4 = (f32[3,4,1024]{2,1,0:T(4,128)S(1)}, f32[3,4,1024]{2,1,0:T(4,128)S(1)}, u32[]{:S(2)}, u32[]{:S(2)}) collective-permute-start(f32[3,4,1024]{2,1,0:T(4,128)S(1)} %get-tuple-element.72), channel_id=1, source_target_pairs={{0,1},{1,2},{2,3},{3,4},{4,5},{5,6},{6,7},{7,8},{8,9},{9,10},{10,1... | collective-permute-start | bytes 147464 | tf_op jit(solution)/shard_map/ppermute | solution.py:27
  56.1 1.6 %copy-start.11 = (f32[1,3,32,1024]{3,2,1,0:T(8,128)S(1)}, f32[1,3,32,1024]{3,2,1,0:T(8,128)}, u32[]{:S(2)}) copy-start(f32[1,3,32,1024]{3,2,1,0:T(8,128)} %param.4) | copy-start | bytes 1179652
  56.1 1.6 %copy-start.50 = (f32[3,32,1024]{2,1,0:T(8,128)S(1)}, f32[3,32,1024]{2,1,0:T(8,128)}, u32[]{:S(2)}) copy-start(f32[3,32,1024]{2,1,0:T(8,128)} %param.5) | copy-start | bytes 1179652
  56.1 5.8 %collective-permute-start.5 = (f32[3,4,1024]{2,1,0:T(4,128)S(1)}, f32[3,4,1024]{2,1,0:T(4,128)S(1)}, u32[]{:S(2)}, u32[]{:S(2)}) collective-permute-start(f32[3,4,1024]{2,1,0:T(4,128)S(1)} %get-tuple-element.73), channel_id=1, source_target_pairs={{1,0},{2,1},{3,2},{4,3},{5,4},{6,5},{7,6},{8,7},{9,8},{10,9},{11,1... | collective-permute-start | bytes 147464 | tf_op jit(solution)/shard_map/ppermute | solution.py:29
  62.6 65.9 %copy-start.34 = (f32[3,32,1024]{2,1,0:T(8,128)}, f32[3,32,1024]{2,1,0:T(8,128)S(1)}, u32[]{:S(2)}) copy-start(f32[3,32,1024]{2,1,0:T(8,128)S(1)} %get-tuple-element.23) | copy-start | bytes 1179652
  128.4 15.7 %copy-start.25 = (f32[1,32,1024]{2,1,0:T(8,128)S(1)}, f32[1,32,1024]{2,1,0:T(8,128)}, u32[]{:S(2)}) copy-start(f32[1,32,1024]{2,1,0:T(8,128)} %copy-done.23) | copy-start | bytes 393220
  128.4 15.7 %copy-start.28 = (f32[1,32,1024]{2,1,0:T(8,128)S(1)}, f32[1,32,1024]{2,1,0:T(8,128)}, u32[]{:S(2)}) copy-start(f32[1,32,1024]{2,1,0:T(8,128)} %copy-done.26) | copy-start | bytes 393220
  128.4 15.7 %copy-start.31 = (f32[1,32,1024]{2,1,0:T(8,128)S(1)}, f32[1,32,1024]{2,1,0:T(8,128)}, u32[]{:S(2)}) copy-start(f32[1,32,1024]{2,1,0:T(8,128)} %copy-done.29) | copy-start | bytes 393220
  128.4 15.7 %copy-start.60 = (f32[32]{0:T(128)S(1)}, f32[32]{0:T(128)}, u32[]{:S(2)}) copy-start(f32[32]{0:T(128)} %and_convert_fusion) | copy-start | bytes 388
  128.5 15.6 %collective-permute-start.6 = (f32[3,32,1024]{2,1,0:T(8,128)S(1)}, f32[3,32,1024]{2,1,0:T(8,128)S(1)}, u32[]{:S(2)}, u32[]{:S(2)}) collective-permute-start(f32[3,32,1024]{2,1,0:T(8,128)S(1)} %divide_subtract_fusion), channel_id=1, source_target_pairs={{16,0},{32,16},{48,32},{64,48},{80,64},{96,80},{112,96},{128,112},... | collective-permute-start | bytes 1179656 | tf_op jit(solution)/shard_map/ppermute | solution.py:39
  (42 other events, 41.4 us)
where the time goes:
time: 146 us; the launch traced here: 145 us
  blocking collectives  65.1 us (45%)
  other arithmetic  23.9 us (16%)
  starting transfers between devices  20.6 us (14%)
  waiting for transfers between devices  15.2 us (10%)
  local copies, waits for them, and re-layouts  14.5 us (10%)
  between operations  5.63 us (4%)
    psum x5, blocking collectives, by_axis(): x = lax.psum(x, axis)  65.1 us
    ppermute x3, waiting for transfers between devices, from_behind(): return lax.ppermute(block, axis, route)  13.4 us
    ppermute x3, starting transfers between devices, from_behind(): return lax.ppermute(block, axis, route)  11.7 us
    unnamed x134, local copies, waits for them, and re-layouts  9.05 us
    ppermute x2, starting transfers between devices, extended_2(): lax.ppermute(tail, axis, [(i, (i + 1) % count) for i in range(ends)])  6.17 us
    add x4, other arithmetic, advance(): merid - half * (north[0] - south[0]) - coriolis * zonal  3.31 us
    mul x8, other arithmetic, section_rows(): return advance(current, coriolis_rows(index, total)) * valid  2.94 us
  transfers between devices with their start and end apart: 7, of which 2 were waited for; matrix products, arithmetic and copies ran while one was open for 19% of the time, Pallas kernels for 0%

commit v1 on v0

--- a/solution.py
+++ b/solution.py
@@ -41,7 +41,7 @@
 
 def by_axis(x, axes):
     for axis in axes:
-        x = lax.psum(x, axis)
+        x = jnp.sum(lax.all_gather(x, axis), axis=0)
     return x
 
 

time: 146 us -> 168 us (1.15)
  local copies, waits for them, and re-layouts: 14.5 us -> 34 us
  other arithmetic: 23.9 us -> 30.1 us
  waiting for transfers between devices: 15.2 us -> 12.5 us
  blocking collectives: 65.1 us -> 63.1 us
    psum x5 -> x0, blocking collectives: 65.1 us -> none  [by_axis(): x = lax.psum(x, axis)]
    unnamed x0 -> x5, blocking collectives: none -> 63.1 us
    unnamed x134 -> x159, local copies, waits for them, and re-layouts: 9.05 us -> 28.5 us
    reduce_sum x0 -> x10, other arithmetic: none -> 6.21 us  [by_axis(): x = jnp.sum(lax.all_gather(x, axis), axis=0)]
    ppermute x2, waiting for transfers between devices: 1.82 us -> 0.01 us  [extended_2(): lax.ppermute(head, axis, [((i + 1) % count, i) for i in range(ends)])]
  transfers between devices with their start and end apart: 7 -> 7, of which waited for: 2 -> 1; matrix products, arithmetic and copies ran while one was open for 19% -> 19% of each run, Pallas kernels for 0% -> 0%
where the time goes in v1:
time: 168 us; the launch traced here: 166 us
  blocking collectives  63.1 us (38%)
  local copies, waits for them, and re-layouts  34 us (20%)
  other arithmetic  30.1 us (18%)
  starting transfers between devices  21 us (12%)
  waiting for transfers between devices  12.5 us (7%)
  between operations  5.72 us (3%)
    unnamed x5, blocking collectives  63.1 us
    unnamed x159, local copies, waits for them, and re-layouts  28.5 us
    ppermute x3, waiting for transfers between devices, from_behind(): return lax.ppermute(block, axis, route)  12.5 us
    ppermute x3, starting transfers between devices, from_behind(): return lax.ppermute(block, axis, route)  12 us
    ppermute x2, starting transfers between devices, extended_2(): lax.ppermute(tail, axis, [(i, (i + 1) % count) for i in range(ends)])  6.38 us
    reduce_sum x10, other arithmetic, by_axis(): x = jnp.sum(lax.all_gather(x, axis), axis=0)  6.21 us
  transfers between devices with their start and end apart: 7, of which 1 were waited for; matrix products, arithmetic and copies ran while one was open for 19% of the time, Pallas kernels for 0%

profile of v1, /device:TPU:16, one launch (start us, length us, event | category | flops | bytes accessed | tf_op | source)
XLA Modules:
  0.0 166.4 jit_solution(9054715374704396468)
XLA Ops:
  0.6 7.6 %collective-permute-start.3 = (f32[3,32,1024]{2,1,0:T(8,128)}, f32[3,32,1024]{2,1,0:T(8,128)}, u32[]{:S(2)}, u32[]{:S(2)}) collective-permute-start(f32[3,32,1024]{2,1,0:T(8,128)} %bitcast.107), channel_id=1, source_target_pairs={{16,0},{32,16},{48,32},{64,48},{80,64},{96,80},{112,96},{128,112},... | collective-permute-start | bytes 1179656 | tf_op jit(solution)/shard_map/ppermute | solution.py:39
  9.2 1.3 collective-permute-start.1
  10.5 3.0 %collective-permute-start = (f32[3,4,1024]{2,1,0:T(4,128)S(1)}, f32[3,4,1024]{2,1,0:T(4,128)S(1)}, u32[]{:S(2)}, u32[]{:S(2)}) collective-permute-start(f32[3,4,1024]{2,1,0:T(4,128)S(1)} %get-tuple-element.254), channel_id=1, source_target_pairs={{0,1},{1,2},{2,3},{3,4},{4,5},{5,6},{6,7},{7,8},{8,9},{9,10},{10,1... | collective-permute-start | bytes 147464 | tf_op jit(solution)/shard_map/ppermute | solution.py:27
  14.4 1.9 %convert_multiply_fusion = f32[1,4,32,1024]{3,2,1,0:T(8,128)} fusion(s32[1,4,32,1024]{3,2,1,0:T(8,128)} %param.7), kind=kLoop, calls=%fused_computation.32 | loop fusion | flops 262144 | bytes 1048576 | tf_op jit(solution)/shard_map/mul | solution.py:144
  16.8 1.3 dynamic-slice
  18.1 1.3 dynamic-slice.1
  28.9 1.9 %collective-permute-start.2 = (f32[3,32,1024]{2,1,0:T(8,128)}, f32[3,32,1024]{2,1,0:T(8,128)}, u32[]{:S(2)}, u32[]{:S(2)}) collective-permute-start(f32[3,32,1024]{2,1,0:T(8,128)} %maximum_multiply_fusion.3), channel_id=1, source_target_pairs={{0,16},{16,32},{32,48},{48,64},{64,80},{80,96},{96,112},{112,128},... | collective-permute-start | bytes 1179656 | tf_op jit(solution)/shard_map/ppermute | solution.py:39
  30.9 2.4 %fusion.50 = (f32[]{:T(128)}, f32[]{:T(128)}, f32[]{:T(128)}, f32[]{:T(128)}, f32[32,1024]{1,0:T(8,128)}, /*index=5*/f32[32,1024]{1,0:T(8,128)S(1)}, f32[32,1024]{1,0:T(8,128)S(1)}) fusion(f32[3,32,1024]{2,1,0:T(8,128)} %maximum_multiply_fusion.3, f32[1,4,32,1024]{3,2,1,0:T(8,128)S(1)} %copy-done.12, f32[1,4,32,1024]{3,2,1,0:T(8,128)S(1)} %copy-done.43, ...), kind=kLoop, calls=%fused_computation.234 | loop fusion | flops 524284 | bytes 1966096 | tf_op jit(solution)/shard_map/reduce_sum | solution.py:118
  38.2 1.1 fusion.66
  39.4 1.2 add_multiply_fusion.3
  55.5 1.3 collective-permute-start.5
  56.8 3.3 %collective-permute-start.4 = (f32[3,4,1024]{2,1,0:T(4,128)S(1)}, f32[3,4,1024]{2,1,0:T(4,128)S(1)}, u32[]{:S(2)}, u32[]{:S(2)}) collective-permute-start(f32[3,4,1024]{2,1,0:T(4,128)S(1)} %get-tuple-element.72), channel_id=1, source_target_pairs={{0,1},{1,2},{2,3},{3,4},{4,5},{5,6},{6,7},{7,8},{8,9},{9,10},{10,1... | collective-permute-start | bytes 147464 | tf_op jit(solution)/shard_map/ppermute | solution.py:27
  60.3 1.7 %multiply_reduce_fusion = (f32[]{:T(128)}, f32[3,32,1024]{2,1,0:T(8,128)S(1)}) fusion(f32[3,32,1024]{2,1,0:T(8,128)S(1)} %copy-done.50, f32[3,32,1024]{2,1,0:T(8,128)} %collective-permute-done.2, pred[]{:T(512)S(6)} %eq.8, f32[1,3,32,1024]{3,2,1,0:T(8,128)S(1)} %copy-done.11), kind=kLoop, calls=%fused_computation.101 | loop fusion | flops 393215 | bytes 1572869 | tf_op jit(solution)/shard_map/reduce_sum | solution.py:152
  63.4 1.4 dynamic-update-slice
  65.6 35.2 %all-reduce.147 = (f32[16]{0:T(128)S(1)}, f32[16]{0:T(128)S(1)}) all-reduce(f32[16]{0:T(128)S(1)} %dynamic-update-slice, f32[16]{0:T(128)S(1)} %dynamic-update-slice.5), channel_id=1, replica_groups=mesh['tm_0'=16,'tm_1'=2,'lat_0'=4,'lat_1'=2,'lat_2'=2] {'tm_0'}, use_global_device_ids=true, to_apply=%add.137 | all-reduce | flops 32 | bytes 256
  102.0 1.3 dynamic-update-slice.1
  103.3 1.3 dynamic-update-slice.6
  104.6 1.3 dynamic-slice.2
  105.9 6.4 %all-reduce.151 = (f32[2]{0:T(128)S(1)}, f32[2]{0:T(128)S(1)}) all-reduce(f32[2]{0:T(128)S(1)} %dynamic-update-slice.1, f32[2]{0:T(128)S(1)} %dynamic-update-slice.6), channel_id=1, replica_groups=mesh['tm_0'=16,'tm_1'=2,'lat_0'=4,'lat_1'=2,'lat_2'=2] {'tm_1'}, use_global_device_ids=true, to_apply=%add.138 | all-reduce | flops 4 | bytes 32
  113.6 1.4 dynamic-update-slice.2
  115.0 1.4 dynamic-update-slice.7
  116.4 1.3 dynamic-slice.3
  117.6 14.1 %all-reduce.148 = (f32[4]{0:T(128)S(1)}, f32[4]{0:T(128)S(1)}) all-reduce(f32[4]{0:T(128)S(1)} %dynamic-update-slice.2, f32[4]{0:T(128)S(1)} %dynamic-update-slice.7), channel_id=1, replica_groups=mesh['tm_0'=16,'tm_1'=2,'lat_0'=4,'lat_1'=2,'lat_2'=2] {'lat_0'}, use_global_device_ids=true, to_apply=%add.139 | all-reduce | flops 8 | bytes 64
  133.0 1.4 dynamic-update-slice.3
  134.4 1.4 dynamic-update-slice.8
  135.8 1.3 dynamic-slice.4
  137.1 4.9 %all-reduce.150 = (f32[2]{0:T(128)S(1)}, f32[2]{0:T(128)S(1)}) all-reduce(f32[2]{0:T(128)S(1)} %dynamic-update-slice.3, f32[2]{0:T(128)S(1)} %dynamic-update-slice.8), channel_id=1, replica_groups=mesh['tm_0'=16,'tm_1'=2,'lat_0'=4,'lat_1'=2,'lat_2'=2] {'lat_1'}, use_global_device_ids=true, to_apply=%add.140 | all-reduce | flops 4 | bytes 32
  143.3 1.4 dynamic-update-slice.4
  144.7 1.4 dynamic-update-slice.9
  146.1 2.4 %all-reduce.149 = (f32[2]{0:T(128)S(1)}, f32[2]{0:T(128)S(1)}) all-reduce(f32[2]{0:T(128)S(1)} %dynamic-update-slice.4, f32[2]{0:T(128)S(1)} %dynamic-update-slice.9), channel_id=1, replica_groups=mesh['tm_0'=16,'tm_1'=2,'lat_0'=4,'lat_1'=2,'lat_2'=2] {'lat_2'}, use_global_device_ids=true, to_apply=%add.141 | all-reduce | flops 4 | bytes 32
  149.9 2.5 %collective-permute-start.6 = (f32[3,32,1024]{2,1,0:T(8,128)S(1)}, f32[3,32,1024]{2,1,0:T(8,128)S(1)}, u32[]{:S(2)}, u32[]{:S(2)}) collective-permute-start(f32[3,32,1024]{2,1,0:T(8,128)S(1)} %divide_subtract_fusion), channel_id=1, source_target_pairs={{16,0},{32,16},{48,32},{64,48},{80,64},{96,80},{112,96},{128,112},... | collective-permute-start | bytes 1179656 | tf_op jit(solution)/shard_map/ppermute | solution.py:39
  153.1 12.5 %collective-permute-done.6 = f32[3,32,1024]{2,1,0:T(8,128)S(1)} collective-permute-done((f32[3,32,1024]{2,1,0:T(8,128)S(1)}, f32[3,32,1024]{2,1,0:T(8,128)S(1)}, u32[]{:S(2)}, u32[]{:S(2)}) %collective-permute-start.6) | collective-permute-done | bytes 393248 | tf_op jit(solution)/shard_map/ppermute | solution.py:39
  (246 shorter events, 37.0 us)
Async XLA Ops:
  0.6 38.7 %collective-permute-start.3 = (f32[3,32,1024]{2,1,0:T(8,128)}, f32[3,32,1024]{2,1,0:T(8,128)}, u32[]{:S(2)}, u32[]{:S(2)}) collective-permute-start(f32[3,32,1024]{2,1,0:T(8,128)} %bitcast.107), channel_id=1, source_target_pairs={{16,0},{32,16},{48,32},{64,48},{80,64},{96,80},{112,96},{128,112},... | collective-permute-start | bytes 1179656 | tf_op jit(solution)/shard_map/ppermute | solution.py:39
  9.2 10.2 %collective-permute-start.1 = (f32[3,4,1024]{2,1,0:T(4,128)S(1)}, f32[3,4,1024]{2,1,0:T(4,128)S(1)}, u32[]{:S(2)}, u32[]{:S(2)}) collective-permute-start(f32[3,4,1024]{2,1,0:T(4,128)S(1)} %get-tuple-element.255), channel_id=1, source_target_pairs={{1,0},{2,1},{3,2},{4,3},{5,4},{6,5},{7,6},{8,7},{9,8},{10,9},{11,1... | collective-permute-start | bytes 147464 | tf_op jit(solution)/shard_map/ppermute | solution.py:29
  10.5 8.9 %collective-permute-start = (f32[3,4,1024]{2,1,0:T(4,128)S(1)}, f32[3,4,1024]{2,1,0:T(4,128)S(1)}, u32[]{:S(2)}, u32[]{:S(2)}) collective-permute-start(f32[3,4,1024]{2,1,0:T(4,128)S(1)} %get-tuple-element.254), channel_id=1, source_target_pairs={{0,1},{1,2},{2,3},{3,4},{4,5},{5,6},{6,7},{7,8},{8,9},{9,10},{10,1... | collective-permute-start | bytes 147464 | tf_op jit(solution)/shard_map/ppermute | solution.py:27
  13.6 7.7 %copy-start.61 = (f32[38]{0:T(128)}, f32[38]{0:T(128)S(1)}, u32[]{:S(2)}) copy-start(f32[38]{0:T(128)S(1)} %and_convert_fusion.3) | copy-start | bytes 460
  13.7 9.4 %copy-start.52 = (f32[36]{0:T(128)}, f32[36]{0:T(128)S(1)}, u32[]{:S(2)}) copy-start(f32[36]{0:T(128)S(1)} %sine_multiply_fusion.2) | copy-start | bytes 436
  13.7 9.6 %copy-start.63 = (f32[36]{0:T(128)}, f32[36]{0:T(128)S(1)}, u32[]{:S(2)}) copy-start(f32[36]{0:T(128)S(1)} %and_convert_fusion.2) | copy-start | bytes 436
  13.8 11.3 %copy-start.54 = (f32[34]{0:T(128)}, f32[34]{0:T(128)S(1)}, u32[]{:S(2)}) copy-start(f32[34]{0:T(128)S(1)} %sine_multiply_fusion.1) | copy-start | bytes 412
  13.8 11.5 %copy-start.65 = (f32[34]{0:T(128)}, f32[34]{0:T(128)S(1)}, u32[]{:S(2)}) copy-start(f32[34]{0:T(128)S(1)} %and_convert_fusion.1) | copy-start | bytes 412
  14.4 5.0 %copy-start.10 = (f32[1,3,32,1024]{3,2,1,0:T(8,128)S(1)}, f32[1,3,32,1024]{3,2,1,0:T(8,128)}, u32[]{:S(2)}) copy-start(f32[1,3,32,1024]{3,2,1,0:T(8,128)} %param.4) | copy-start | bytes 1179652
  19.6 1.5 copy-start.13
  21.5 1.6 copy-start.15
  21.5 1.5 copy-start.17
  21.7 1.3 copy-start
  23.5 1.6 copy-start.19
  23.5 1.5 copy-start.21
  23.7 1.3 copy-start.2
  25.5 1.9 %copy-start.32 = (f32[3,32,1]{2,1,0:T(8,128)}, f32[3,32,1]{2,1,0:T(8,128)S(1)}, u32[]{:S(2)}) copy-start(f32[3,32,1]{2,1,0:T(8,128)S(1)} %get-tuple-element.216) | copy-start | bytes 1156
  25.7 1.7 %copy-start.6 = (f32[3,32,1023]{2,1,0:T(8,128)}, f32[3,32,1023]{2,1,0:T(8,128)S(1)}, u32[]{:S(2)}) copy-start(f32[3,32,1023]{2,1,0:T(8,128)S(1)} %get-tuple-element.213) | copy-start | bytes 1178500
  25.7 1.7 %copy-start.8 = (f32[3,32,1023]{2,1,0:T(8,128)}, f32[3,32,1023]{2,1,0:T(8,128)S(1)}, u32[]{:S(2)}) copy-start(f32[3,32,1023]{2,1,0:T(8,128)S(1)} %get-tuple-element.214) | copy-start | bytes 1178500
  27.5 3.4 %copy-start.43 = (f32[1,4,32,1024]{3,2,1,0:T(8,128)S(1)}, f32[1,4,32,1024]{3,2,1,0:T(8,128)}, u32[]{:S(2)}) copy-start(f32[1,4,32,1024]{3,2,1,0:T(8,128)} %param.6) | copy-start | bytes 1572868
  27.6 3.2 %copy-start.12 = (f32[1,4,32,1024]{3,2,1,0:T(8,128)S(1)}, f32[1,4,32,1024]{3,2,1,0:T(8,128)}, u32[]{:S(2)}) copy-start(f32[1,4,32,1024]{3,2,1,0:T(8,128)} %convert_multiply_fusion) | copy-start | bytes 1572868
  28.9 31.4 %collective-permute-start.2 = (f32[3,32,1024]{2,1,0:T(8,128)}, f32[3,32,1024]{2,1,0:T(8,128)}, u32[]{:S(2)}, u32[]{:S(2)}) collective-permute-start(f32[3,32,1024]{2,1,0:T(8,128)} %maximum_multiply_fusion.3), channel_id=1, source_target_pairs={{0,16},{16,32},{32,48},{48,64},{64,80},{80,96},{96,112},{112,128},... | collective-permute-start | bytes 1179656 | tf_op jit(solution)/shard_map/ppermute | solution.py:39
  55.5 7.2 %collective-permute-start.5 = (f32[3,4,1024]{2,1,0:T(4,128)S(1)}, f32[3,4,1024]{2,1,0:T(4,128)S(1)}, u32[]{:S(2)}, u32[]{:S(2)}) collective-permute-start(f32[3,4,1024]{2,1,0:T(4,128)S(1)} %get-tuple-element.73), channel_id=1, source_target_pairs={{1,0},{2,1},{3,2},{4,3},{5,4},{6,5},{7,6},{8,7},{9,8},{10,9},{11,1... | collective-permute-start | bytes 147464 | tf_op jit(solution)/shard_map/ppermute | solution.py:29
  56.8 3.5 %copy-start.11 = (f32[1,3,32,1024]{3,2,1,0:T(8,128)S(1)}, f32[1,3,32,1024]{3,2,1,0:T(8,128)}, u32[]{:S(2)}) copy-start(f32[1,3,32,1024]{3,2,1,0:T(8,128)} %param.4) | copy-start | bytes 1179652
  56.8 3.5 %copy-start.50 = (f32[3,32,1024]{2,1,0:T(8,128)S(1)}, f32[3,32,1024]{2,1,0:T(8,128)}, u32[]{:S(2)}) copy-start(f32[3,32,1024]{2,1,0:T(8,128)} %param.5) | copy-start | bytes 1179652
  56.8 5.9 %collective-permute-start.4 = (f32[3,4,1024]{2,1,0:T(4,128)S(1)}, f32[3,4,1024]{2,1,0:T(4,128)S(1)}, u32[]{:S(2)}, u32[]{:S(2)}) collective-permute-start(f32[3,4,1024]{2,1,0:T(4,128)S(1)} %get-tuple-element.72), channel_id=1, source_target_pairs={{0,1},{1,2},{2,3},{3,4},{4,5},{5,6},{6,7},{7,8},{8,9},{9,10},{10,1... | collective-permute-start | bytes 147464 | tf_op jit(solution)/shard_map/ppermute | solution.py:27
  63.4 86.5 %copy-start.34 = (f32[3,32,1024]{2,1,0:T(8,128)}, f32[3,32,1024]{2,1,0:T(8,128)S(1)}, u32[]{:S(2)}) copy-start(f32[3,32,1024]{2,1,0:T(8,128)S(1)} %get-tuple-element.23) | copy-start | bytes 1179652
  149.8 15.7 %copy-start.25 = (f32[1,32,1024]{2,1,0:T(8,128)S(1)}, f32[1,32,1024]{2,1,0:T(8,128)}, u32[]{:S(2)}) copy-start(f32[1,32,1024]{2,1,0:T(8,128)} %copy-done.23) | copy-start | bytes 393220
  149.8 15.7 %copy-start.28 = (f32[1,32,1024]{2,1,0:T(8,128)S(1)}, f32[1,32,1024]{2,1,0:T(8,128)}, u32[]{:S(2)}) copy-start(f32[1,32,1024]{2,1,0:T(8,128)} %copy-done.26) | copy-start | bytes 393220
  149.8 15.7 %copy-start.31 = (f32[1,32,1024]{2,1,0:T(8,128)S(1)}, f32[1,32,1024]{2,1,0:T(8,128)}, u32[]{:S(2)}) copy-start(f32[1,32,1024]{2,1,0:T(8,128)} %copy-done.29) | copy-start | bytes 393220
  149.9 15.6 %collective-permute-start.6 = (f32[3,32,1024]{2,1,0:T(8,128)S(1)}, f32[3,32,1024]{2,1,0:T(8,128)S(1)}, u32[]{:S(2)}, u32[]{:S(2)}) collective-permute-start(f32[3,32,1024]{2,1,0:T(8,128)S(1)} %divide_subtract_fusion), channel_id=1, source_target_pairs={{16,0},{32,16},{48,32},{64,48},{80,64},{96,80},{112,96},{128,112},... | collective-permute-start | bytes 1179656 | tf_op jit(solution)/shard_map/ppermute | solution.py:39
  152.5 13.1 %copy-start.60 = (f32[32]{0:T(128)S(1)}, f32[32]{0:T(128)}, u32[]{:S(2)}) copy-start(f32[32]{0:T(128)} %and_convert_fusion) | copy-start | bytes 388
  (42 other events, 41.3 us)
